TPU v7x, 32 devices: a whole 2x2x4 slice. The times are simulated.
32 devices in a mesh: task: 4 (over x, core), dp: 8 (over z, y).
Axes of the slice: x: 2, y: 2, z: 4, core: 2. Of those that a mesh axis runs over, the one named last changes fastest.
Arguments:
- inputs: bfloat16 [8192, 4096], P('dp'), may hold values from -6 to 6
- cotangent: bfloat16 [4, 8192, 1024], P('task', 'dp'), may hold values from -0.44194174 to 0.44194174
- task_order: int32 [4], replicated, may hold values from 0 to 3, each once
- conflict_flags: int32 [4, 4], replicated, may hold values 0 or 1
Outputs:
- combined: bfloat16 [4096, 1024], P(None, 'task')
Inputs may be any that keep to these rules, and one draw needn't show every extreme that they name: `task_order`: a permutation of the tasks. `conflict_flags`: diagonal entries are ignored.
All inputs are finite; a program needn't handle non-finite values.
Results may differ from a plain program's by a relative error of at most 0.001.
Values may be sent and summed in bfloat16 or wider, within the bound.
A program may use at most 128 MiB of HBM per device.

v0:
```python
import functools

import jax
import jax.numpy as jnp
from jax import lax
from jax.experimental import pallas as pl
from jax.experimental.pallas import tpu as pltpu
from jax.sharding import PartitionSpec as P

MESH = pl.DeviceIdType.MESH
TOP = 32767.0


def coded(tile):
    high = jnp.maximum(jnp.max(jnp.abs(tile), axis=0, keepdims=True), 1e-30)
    code = jnp.round(tile * (TOP / high)).astype(jnp.int32).astype(jnp.int16)
    return code, high * (1.0 / TOP)


def decoded(code, scale):
    return code.astype(jnp.int32).astype(jnp.float32) * scale


def kernel(tasks, ndp, chunks, halves, order_ref, flags_ref, x_ref, c_ref, out_ref,
           ysend, yscale, yrecv, yrscale, zsend, zscale, zrecv, zrscale, own, cots,
           gsend, grads, gram_own, gram_dp, gram_mid, gram_task,
           ys_sem, yr_sem, zs_sem, zr_sem, ts_sem, tr_sem, gs_sem, gr_sem,
           hs_sem, hr_sem, as_sem, ar_sem):
    nz = ndp // 2
    me_t = lax.axis_index("task")
    me_d = lax.axis_index("dp")
    z = me_d // 2
    y = me_d % 2
    rows = x_ref.shape[1] // ndp
    step = rows * halves // chunks
    width = c_ref.shape[1] // tasks
    part = width // halves

    def zof(k):
        return lax.rem(z + k, nz)

    def dp_at(zi, yi):
        return zi * 2 + yi

    partner = (me_t, dp_at(z, 1 - y))

    barrier = pltpu.get_barrier_semaphore()
    for k in range(1, ndp):
        pl.semaphore_signal(barrier, inc=1, device_id=(me_t, lax.rem(me_d + k, ndp)), device_id_type=MESH)
    for k in range(1, tasks):
        pl.semaphore_signal(barrier, inc=1, device_id=(lax.rem(me_t + k, tasks), me_d), device_id_type=MESH)
    pl.semaphore_wait(barrier, ndp + tasks - 2)

    def send(src, dst, s, r, device):
        copy = pltpu.make_async_remote_copy(src_ref=src, dst_ref=dst, send_sem=s, recv_sem=r,
                                            device_id=device, device_id_type=MESH)
        copy.start()
        return copy

    def product(zi, yi, c):
        first = pl.multiple_of(dp_at(zi, yi) * rows + c // halves * step, step)
        return lax.dot_general(x_ref[:, pl.ds(first, step)], cots[c % halves], (((0,), (0,)), ((), ())),
                               preferred_element_type=jnp.float32)

    for h in range(halves):
        for t in range(tasks):
            cots[h, :, t * part:(t + 1) * part] = c_ref[:, t * width + h * part:t * width + (h + 1) * part]

    ycopies, zcopies, tcopies = {}, {}, {}
    for c in range(chunks):
        def fill(k, carry, c=c):
            code, scale = coded(product(zof(k), 1 - y, c))
            ysend[c, k] = code
            yscale[c, k] = scale
            return carry
        lax.fori_loop(0, nz, fill, 0)
        ycopies[c] = (send(ysend.at[c], yrecv.at[c], ys_sem.at[c, 0], yr_sem.at[c, 0], partner),
                      send(yscale.at[c], yrscale.at[c], ys_sem.at[c, 1], yr_sem.at[c, 1], partner))

    def second(c):
        for copy in ycopies[c]:
            copy.wait_recv()
        zcopies[c] = []
        for k in [*range(nz - 1, 0, -1), 0]:
            total = product(zof(k), y, c) + decoded(yrecv[c, k], yrscale[c, k])
            if k == 0:
                own[c] = total
            else:
                code, scale = coded(total)
                zsend[c, k] = code
                zscale[c, k] = scale
                peer = (me_t, dp_at(zof(k), y))
                zcopies[c] += [send(zsend.at[c, k], zrecv.at[c, k], zs_sem.at[c, k, 0], zr_sem.at[c, k, 0], peer),
                               send(zscale.at[c, k], zrscale.at[c, k], zs_sem.at[c, k, 1], zr_sem.at[c, k, 1], peer)]

    def third(c):
        for copy in zcopies[c]:
            copy.wait_recv()
        total = own[c]
        for k in range(1, nz):
            total = total + decoded(zrecv[c, k], zrscale[c, k])
        for t in range(tasks):
            gsend[c, t] = total[:, t * part:(t + 1) * part]
        grads[me_t, c] = gsend[c, me_t]
        tcopies[c] = []
        for k in range(1, tasks):
            peer = lax.rem(me_t + k, tasks)
            tcopies[c].append(send(gsend.at[c, peer], grads.at[me_t, c], ts_sem.at[c, k], tr_sem.at[c, k],
                                   (peer, me_d)))

    pairs = [(s, t) for s in range(tasks) for t in range(s, tasks)]
    sums = {pair: jnp.zeros((8, part), jnp.float32) for pair in pairs}

    def fourth(c):
        for copy in tcopies[c]:
            copy.wait_recv()
        held = [grads[t, c] for t in range(tasks)]
        for s, t in pairs:
            both = held[s] * held[t]
            sums[s, t] = sums[s, t] + jnp.sum(both.reshape(step // 8, 8, part), axis=0)

    for c in range(chunks + 2):
        if c < chunks:
            second(c)
        if 0 <= c - 1 < chunks:
            third(c - 1)
        if c >= 2:
            fourth(c - 2)

    line = lax.broadcasted_iota(jnp.int32, (8, 128), 0)
    lane = lax.broadcasted_iota(jnp.int32, (8, 128), 1)
    gram = jnp.zeros((8, 128), jnp.float32)
    for s, t in pairs:
        value = jnp.sum(jnp.sum(sums[s, t], axis=0, keepdims=True), axis=1, keepdims=True)
        here = ((line == s) & (lane == t)) | ((line == t) & (lane == s))
        gram = gram + jnp.where(here, value, 0.0)

    def swap(value, buffer_own, buffer, count, s_sem, r_sem, device):
        buffer_own[...] = value
        copies = [send(buffer_own, buffer.at[k], s_sem.at[k], r_sem.at[k], device(k)) for k in range(1, count)]
        for k, copy in enumerate(copies, 1):
            copy.wait_recv()
            value = value + buffer[k]
        for copy in copies:
            copy.wait_send()
        return value

    gram = swap(gram, gram_own, gram_dp, ndp, gs_sem, gr_sem, lambda k: (me_t, lax.rem(me_d + k, ndp)))
    gram = swap(gram, gram_mid, gram_task, tasks, hs_sem, hr_sem, lambda k: (lax.rem(me_t + k, tasks), me_d))

    cols = [jnp.sum(jnp.where(lane == m, gram, 0.0), axis=1, keepdims=True) for m in range(tasks)]
    entry = lambda column, i: jnp.sum(jnp.where(line[:, :1] == i, column, 0.0), axis=0, keepdims=True)
    row = line[:, :1]
    coefficients = [(row == m).astype(jnp.float32) for m in range(tasks)]
    flag_cols = []
    for m in range(tasks):
        column = jnp.zeros((8, 1), jnp.float32)
        for i in range(tasks):
            column = column + jnp.where(row == i, flags_ref[i, m].astype(jnp.float32), 0.0)
        flag_cols.append(column)
    for position in range(tasks):
        target = order_ref[position]
        picks = [jnp.where(target == m, 1.0, 0.0) for m in range(tasks)]
        column = sum(cols[m] * picks[m] for m in range(tasks))
        dots = sum(coefficients[m] * entry(column, m) for m in range(tasks))
        square = sum(entry(column, m) * picks[m] for m in range(tasks))
        active = sum(flag_cols[m] * picks[m] for m in range(tasks)) * jnp.where(row == target, 0.0, 1.0)
        removed = jnp.minimum(dots, 0.0) / square * active
        coefficients = [coefficients[m] - removed * picks[m] for m in range(tasks)]
    weights = [jnp.sum(coefficients[m], axis=0, keepdims=True) for m in range(tasks)]

    def block(d):
        return out_ref.at[pl.ds(pl.multiple_of(d * rows, rows), rows), :]

    for c in range(chunks):
        mixed = sum(weights[t] * grads[t, c] for t in range(tasks))
        first = pl.multiple_of(me_d * rows + c // halves * step, step)
        h = c % halves
        out_ref[pl.ds(first, step), h * part:(h + 1) * part] = mixed.astype(jnp.bfloat16)
    mine = block(me_d)
    along = {k: send(mine, mine, as_sem.at[0, k], ar_sem.at[0, k], (me_t, dp_at(zof(k), y)))
             for k in range(1, nz)}
    across = [send(mine, mine, as_sem.at[1, 0], ar_sem.at[1, 0], partner)]
    for k in range(1, nz):
        along[k].wait_recv()
        held = block(dp_at(lax.rem(z + nz - k, nz), y))
        across.append(send(held, held, as_sem.at[1, k], ar_sem.at[1, k], partner))
    for copy in across:
        copy.wait_recv()
    for copy in [*across, *along.values()]:
        copy.wait_send()
    for group in (ycopies, zcopies, tcopies):
        for c in range(chunks):
            for copy in group[c]:
                copy.wait_send()


def solution(mesh):
    tasks, ndp = mesh.shape["task"], mesh.shape["dp"]
    nz = ndp // 2

    def on_device(inputs, cotangent, task_order, conflict_flags):
        cot = cotangent[0]
        rows = inputs.shape[1] // ndp
        step = min(rows, 128)
        width = cot.shape[1] // tasks
        halves = 2 if width % 256 == 0 else 1
        chunks = rows // step * halves
        part = width // halves
        kvw = part * tasks
        vmem, dma = pltpu.VMEM, pltpu.SemaphoreType.DMA
        f32, i16 = jnp.float32, jnp.int16
        scratch = [
            vmem((chunks, nz, step, kvw), i16), vmem((chunks, nz, 1, kvw), f32),
            vmem((chunks, nz, step, kvw), i16), vmem((chunks, nz, 1, kvw), f32),
            vmem((chunks, nz, step, kvw), i16), vmem((chunks, nz, 1, kvw), f32),
            vmem((chunks, nz, step, kvw), i16), vmem((chunks, nz, 1, kvw), f32),
            vmem((chunks, step, kvw), f32), vmem((halves, cot.shape[0], kvw), cot.dtype),
            vmem((chunks, tasks, step, part), f32), vmem((tasks, chunks, step, part), f32),
            vmem((8, 128), f32), vmem((ndp, 8, 128), f32), vmem((8, 128), f32), vmem((tasks, 8, 128), f32),
            dma((chunks, 2)), dma((chunks, 2)), dma((chunks, nz, 2)), dma((chunks, nz, 2)),
            dma((chunks, tasks)), dma((chunks, tasks)), dma((ndp,)), dma((ndp,)),
            dma((tasks,)), dma((tasks,)), dma((2, nz)), dma((2, nz)),
        ]
        smem = pl.BlockSpec(memory_space=pltpu.SMEM)
        whole = pl.BlockSpec(memory_space=pltpu.VMEM)
        return pl.pallas_call(
            functools.partial(kernel, tasks, ndp, chunks, halves),
            out_shape=jax.ShapeDtypeStruct((inputs.shape[1], width), jnp.bfloat16),
            in_specs=[smem, smem, whole, whole],
            out_specs=whole,
            scratch_shapes=scratch,
            compiler_params=pltpu.CompilerParams(collective_id=0, has_side_effects=True,
                                                 vmem_limit_bytes=60 * 1024 * 1024),
        )(task_order, conflict_flags, inputs, cot)

    return jax.shard_map(
        on_device, mesh=mesh,
        in_specs=(P("dp", None), P("task", "dp", None), P(), P()),
        out_specs=P(None, "task"), check_vma=False,
    )
```

profile of v0, /device:TPU:0, one launch (start us, length us, event | category | flops | bytes accessed | tf_op | source)
XLA Modules:
  0.0 166.5 jit_solution(10309919518672502743)
XLA Ops:
  0.0 163.5 %shard_map.46 = bf16[4096,256]{1,0:T(8,128)(2,1)} custom-call(s32[4]{0:T(128)} %order_ref.1, s32[4,4]{1,0:T(4,128)} %flags_ref.1, bf16[1024,4096]{1,0:T(8,128)(2,1)} %x_ref.1, bf16[1024,1024]{1,0:T(8,128)(2,1)} %bitcast.1), custom_call_target="tpu_custom_call" | custom-call | tf_op jit(solution)/shard_map/pallas_call | solution.py:227
  163.5 3.0 %copy.6 = bf16[4096,256]{1,0:T(8,128)(2,1)} copy(bf16[4096,256]{1,0:T(8,128)(2,1)} %shard_map.46) | data formatting | bytes 4194304
where the time goes:
time: 169 us; the launch traced here: 167 us
  Pallas kernels  163 us (96%)
  local copies, waits for them, and re-layouts  3.05 us (2%)
    pallas_call x1, Pallas kernels, on_device(): pl.pallas_call(functools.partial(kernel, tasks, ndp, chunks, halves), out...  163 us

commit v1 on v0

v1 whole, which is shorter than its diff:
```python
import functools

import jax
import jax.numpy as jnp
from jax import lax
from jax.experimental import pallas as pl
from jax.experimental.pallas import tpu as pltpu
from jax.sharding import PartitionSpec as P

MESH = pl.DeviceIdType.MESH
TOP = 32767.0
SHARE = (7, 16)


def coded(tile):
    high = jnp.maximum(jnp.max(jnp.abs(tile), axis=0, keepdims=True), 1e-30)
    code = jnp.round(tile * (TOP / high)).astype(jnp.int32).astype(jnp.int16)
    return code, high * (1.0 / TOP)


def decoded(code, scale):
    return code.astype(jnp.int32).astype(jnp.float32) * scale


def plan(tasks, blocks):
    bounds = [j * blocks * SHARE[0] // SHARE[1] for j in range(tasks + 1)]
    return [bounds[j + 1] - bounds[j] for j in range(tasks)]


def kernel(tasks, ndp, blocks, order_ref, flags_ref, x_hbm, c_hbm, out_ref,
           x_ref, xt, cots, ysend_a, yscale_a, yrecv_a, yrscale_a, zsend_a, zscale_a, zrecv_a, zrscale_a, own_a,
           ysend_b, yscale_b, yrecv_b, yrscale_b, zsend_b, zscale_b, zrecv_b, zrscale_b, own_b,
           grads, gram_own, gram_dp, gram_mid, gram_task,
           x_sem, c_sem, cs_sem, cr_sem,
           yas_sem, yar_sem, zas_sem, zar_sem, ybs_sem, ybr_sem, zbs_sem, zbr_sem,
           gs_sem, gr_sem, hs_sem, hr_sem, ns_sem, nr_sem, ms_sem, mr_sem):
    nz = ndp // 2
    far = nz // 2
    pairs_of = tasks // 2
    me_t = lax.axis_index("task")
    me_d = lax.axis_index("dp")
    z = me_d // 2
    y = me_d % 2
    rows = x_ref.shape[1] // ndp
    step = rows // blocks
    width = cots.shape[2]
    first_y = plan(tasks, blocks)
    first_z = [blocks - n for n in first_y]
    base_y = [sum(first_y[:j]) for j in range(tasks)]
    base_z = [sum(first_z[:j]) for j in range(tasks)]

    def zof(k):
        return lax.rem(z + k + nz, nz)

    def dp_at(zi, yi):
        return zi * 2 + yi

    def mate(j, way):
        return (lax.rem(me_t // 2 + way * (j // 2) + pairs_of, pairs_of) * 2 + lax.rem(me_t % 2 + j % 2, 2))

    partner = (me_t, dp_at(z, 1 - y))

    def remote(src, dst, s, r, device):
        return pltpu.make_async_remote_copy(src_ref=src, dst_ref=dst, send_sem=s, recv_sem=r,
                                            device_id=device, device_id_type=MESH)

    x_copies = []
    for d in range(ndp):
        part = pl.ds(d * rows, rows)
        x_copies.append(pltpu.make_async_copy(x_hbm.at[:, part], x_ref.at[:, part], x_sem.at[d]))
    c_copy = pltpu.make_async_copy(c_hbm.at[:, pl.ds(pl.multiple_of(me_t * width, width), width)], cots.at[0], c_sem)
    c_copy.start()
    for copy in x_copies:
        copy.start()

    barrier = pltpu.get_barrier_semaphore()
    for k in range(1, ndp):
        pl.semaphore_signal(barrier, inc=1, device_id=(me_t, lax.rem(me_d + k, ndp)), device_id_type=MESH)
    for k in range(1, tasks):
        pl.semaphore_signal(barrier, inc=1, device_id=(lax.rem(me_t + k, tasks), me_d), device_id_type=MESH)
    pl.semaphore_wait(barrier, ndp + tasks - 2)

    def c_remote(j):
        peer = mate(j, 1)
        return remote(c_hbm.at[:, pl.ds(pl.multiple_of(peer * width, width), width)], cots.at[j],
                      cs_sem.at[j], cr_sem.at[j], (peer, me_d))

    for j in range(1, tasks):
        c_remote(j).start()
    c_copy.wait()
    for copy in x_copies:
        copy.wait()

    def product(j, block, zi, yi):
        index = dp_at(zi, yi) * blocks + block
        if j == 0:
            turned = x_ref[:, pl.ds(pl.multiple_of(index * step, step), step)].T
            xt[index] = turned
        else:
            turned = xt[index]
        return jnp.dot(turned, cots[j], preferred_element_type=jnp.float32)

    def side(u):
        return 1 - 2 * (u % 2)

    def messages(u):
        sign = side(u)
        chain = [(far - h, sign, h, far - h - 1 if h < far else None) for h in range(far, 0, -1)]
        chain += [(nz - 1 - h, -sign, h, nz - 2 - h if h < far - 1 else None) for h in range(far - 1, 0, -1)]
        return chain

    lasts = [far - 1] + ([nz - 2] if nz > 2 else [])

    def ya(u):
        return (remote(ysend_a.at[u], yrecv_a.at[u], yas_sem.at[u, 0], yar_sem.at[u, 0], partner),
                remote(yscale_a.at[u], yrscale_a.at[u], yas_sem.at[u, 1], yar_sem.at[u, 1], partner))

    def yb(u):
        return (remote(ysend_b.at[u], yrecv_b.at[u], ybs_sem.at[u, 0], ybr_sem.at[u, 0], partner),
                remote(yscale_b.at[u], yrscale_b.at[u], ybs_sem.at[u, 1], ybr_sem.at[u, 1], partner))

    def za(u, m, sign):
        peer = (me_t, dp_at(zof(sign), y))
        return (remote(zsend_a.at[u, m], zrecv_a.at[u, m], zas_sem.at[u, m, 0], zar_sem.at[u, m, 0], peer),
                remote(zscale_a.at[u, m], zrscale_a.at[u, m], zas_sem.at[u, m, 1], zar_sem.at[u, m, 1], peer))

    def zb(u, m, sign):
        peer = (me_t, dp_at(zof(sign), y))
        return (remote(zsend_b.at[u, m], zrecv_b.at[u, m], zbs_sem.at[u, m, 0], zbr_sem.at[u, m, 0], peer),
                remote(zscale_b.at[u, m], zrscale_b.at[u, m], zbs_sem.at[u, m, 1], zbr_sem.at[u, m, 1], peer))

    def start(copies):
        for copy in copies:
            copy.start()

    def arrive(copies):
        for copy in copies:
            copy.wait_recv()

    def each(count, body):
        if count:
            lax.fori_loop(0, count, lambda i, carry: (body(i), carry)[1], 0)

    def a_y(j):
        def unit(i):
            u = base_y[j] + i

            def fill(k):
                code, scale = coded(product(j, i, zof(k), 1 - y))
                ysend_a[u, k] = code
                yscale_a[u, k] = scale
            each(nz, fill)
            start(ya(u))
        each(first_y[j], unit)

    def o_y(j):
        def unit(i):
            u = base_y[j] + i

            def fill(k):
                own_a[u, k] = product(j, i, zof(k), y)
            each(nz, fill)
        each(first_y[j], unit)

    def z_part_b(j, i, message):
        u = base_z[j] + i
        m, sign, h, needs = message
        if needs is not None:
            arrive(zb(u, needs, sign))

        def fill(yi):
            total = product(j, first_y[j] + i, zof(sign * h), yi)
            if needs is not None:
                total = total + decoded(zrecv_b[u, needs, yi], zrscale_b[u, needs, yi])
            code, scale = coded(total)
            zsend_b[u, m, yi] = code
            zscale_b[u, m, yi] = scale
        each(2, fill)
        start(zb(u, m, sign))

    def a_z(j):
        each(first_z[j], lambda i: z_part_b(j, i, messages(base_z[j] + i)[0]))

    def b_z(j):
        def unit(i):
            chain = messages(base_z[j] + i)[1:]
            for message in sorted(chain, key=lambda one: one[3] is not None):
                z_part_b(j, i, message)
        each(first_z[j], unit)

    def c_z(j):
        def unit(i):
            u = base_z[j] + i
            arrive(zb(u, lasts[0], side(u)))
            for m in lasts[1:]:
                arrive(zb(u, m, -side(u)))

            def total(yi):
                value = own_b[u, yi]
                for m in lasts:
                    value = value + decoded(zrecv_b[u, m, yi], zrscale_b[u, m, yi])
                return value
            code, scale = coded(total(1 - y))
            ysend_b[u] = code
            yscale_b[u] = scale
            start(yb(u))
            own_b[u, y] = total(y)
        each(first_z[j], unit)

    def o_z(j):
        def unit(i):
            u = base_z[j] + i

            def fill(yi):
                own_b[u, yi] = product(j, first_y[j] + i, z, yi)
            each(2, fill)
        each(first_z[j], unit)

    def task_of(j):
        return mate(j, -1)

    def f_z(j):
        def unit(i):
            u = base_z[j] + i
            arrive(yb(u))
            grads[task_of(j), first_y[j] + i] = own_b[u, y] + decoded(yrecv_b[u], yrscale_b[u])
        each(first_z[j], unit)

    def z_part_a(u, message):
        m, sign, h, needs = message
        k = lax.rem(sign * h + nz, nz)
        total = own_a[u, k] + decoded(yrecv_a[u, k], yrscale_a[u, k])
        if needs is not None:
            arrive(za(u, needs, sign))
            total = total + decoded(zrecv_a[u, needs], zrscale_a[u, needs])
        code, scale = coded(total)
        zsend_a[u, m] = code
        zscale_a[u, m] = scale
        start(za(u, m, sign))

    def b1_y(j):
        def unit(i):
            u = base_y[j] + i
            arrive(ya(u))
            z_part_a(u, messages(u)[0])
        each(first_y[j], unit)

    def b2_y(j):
        def unit(i):
            u = base_y[j] + i
            for message in sorted(messages(u)[1:], key=lambda one: one[3] is not None):
                z_part_a(u, message)
        each(first_y[j], unit)

    def f_y(j):
        def unit(i):
            u = base_y[j] + i
            arrive(za(u, lasts[0], side(u)))
            for m in lasts[1:]:
                arrive(za(u, m, -side(u)))
            total = own_a[u, 0] + decoded(yrecv_a[u, 0], yrscale_a[u, 0])
            for m in lasts:
                total = total + decoded(zrecv_a[u, m], zrscale_a[u, m])
            grads[task_of(j), i] = total
        each(first_y[j], unit)

    for j in range(tasks):
        if j:
            c_remote(j).wait_recv()
        a_z(j)
        a_y(j)
        b_z(j)
        o_z(j)
        o_y(j)
        if j >= 2:
            c_z(j - 2)
            b1_y(j - 2)
    for j in range(max(tasks - 2, 0), tasks):
        b1_y(j)
        c_z(j)
    for j in range(tasks):
        b2_y(j)
    for j in range(tasks):
        f_z(j)
    for j in range(tasks):
        f_y(j)

    pairs = [(s, t) for s in range(tasks) for t in range(s, tasks)]

    def products(index, sums):
        held = [grads[t, index] for t in range(tasks)]
        return tuple(total + jnp.sum((held[s] * held[t]).reshape(step // 8, 8, width), axis=0)
                     for total, (s, t) in zip(sums, pairs))

    sums = lax.fori_loop(0, blocks, products, tuple(jnp.zeros((8, width), jnp.float32) for _ in pairs))
    line = lax.broadcasted_iota(jnp.int32, (8, 128), 0)
    lane = lax.broadcasted_iota(jnp.int32, (8, 128), 1)
    gram = jnp.zeros((8, 128), jnp.float32)
    for total, (s, t) in zip(sums, pairs):
        value = jnp.sum(jnp.sum(total, axis=0, keepdims=True), axis=1, keepdims=True)
        here = ((line == s) & (lane == t)) | ((line == t) & (lane == s))
        gram = gram + jnp.where(here, value, 0.0)

    def swap(value, buffer_own, buffer, count, s_sem, r_sem, device):
        buffer_own[...] = value
        copies = [remote(buffer_own, buffer.at[k], s_sem.at[k], r_sem.at[k], device(k)) for k in range(1, count)]
        start(copies)
        for k, copy in enumerate(copies, 1):
            copy.wait_recv()
            value = value + buffer[k]
        for copy in copies:
            copy.wait_send()
        return value

    gram = swap(gram, gram_own, gram_dp, ndp, gs_sem, gr_sem, lambda k: (me_t, lax.rem(me_d + k, ndp)))
    gram = swap(gram, gram_mid, gram_task, tasks, hs_sem, hr_sem, lambda k: (lax.rem(me_t + k, tasks), me_d))

    cols = [jnp.sum(jnp.where(lane == m, gram, 0.0), axis=1, keepdims=True) for m in range(tasks)]
    entry = lambda column, i: jnp.sum(jnp.where(line[:, :1] == i, column, 0.0), axis=0, keepdims=True)
    row = line[:, :1]
    coefficients = [(row == m).astype(jnp.float32) for m in range(tasks)]
    flag_cols = []
    for m in range(tasks):
        column = jnp.zeros((8, 1), jnp.float32)
        for i in range(tasks):
            column = column + jnp.where(row == i, flags_ref[i, m].astype(jnp.float32), 0.0)
        flag_cols.append(column)
    for position in range(tasks):
        target = order_ref[position]
        picks = [jnp.where(target == m, 1.0, 0.0) for m in range(tasks)]
        column = sum(cols[m] * picks[m] for m in range(tasks))
        dots = sum(coefficients[m] * entry(column, m) for m in range(tasks))
        square = sum(entry(column, m) * picks[m] for m in range(tasks))
        active = sum(flag_cols[m] * picks[m] for m in range(tasks)) * jnp.where(row == target, 0.0, 1.0)
        removed = jnp.minimum(dots, 0.0) / square * active
        coefficients = [coefficients[m] - removed * picks[m] for m in range(tasks)]
    weights = [jnp.sum(coefficients[m], axis=0, keepdims=True) for m in range(tasks)]

    half = rows // 2

    def segment(zi, yi, part, which):
        size = half if which is None else half // 2
        first = dp_at(zi, yi) * rows + part * half + (0 if which is None else which * size)
        return out_ref.at[pl.ds(pl.multiple_of(first, size), size), :]

    def mix(index, carry):
        mixed = sum(weights[t] * grads[t, index] for t in range(tasks))
        out_ref[pl.ds(pl.multiple_of(me_d * rows + index * step, step), step), :] = mixed.astype(jnp.bfloat16)
        return carry
    lax.fori_loop(0, blocks, mix, 0)

    def item(i):
        return (y, i) if i < 2 else (1 - y, 1)

    def hop(i, way, h, source=True):
        sign = 1 - 2 * way
        yi, part = item(i)
        which = way if h == far else None
        ref = segment(zof(-sign * (h - 1)), yi, part, which)
        return remote(ref, ref, ns_sem.at[i, way, h], nr_sem.at[i, way, h], (me_t, dp_at(zof(sign), y)))

    def cross(index, zi, part, which):
        ref = segment(zi, y, part, which)
        return remote(ref, ref, ms_sem.at[index], mr_sem.at[index], partner)

    zcopies, ycopies = [], []

    def go(copy, group):
        copy.start()
        group.append(copy)
        return copy

    got = {}
    second = go(cross(0, z, 1, None), ycopies)
    for i in (0, 1):
        for way in (0, 1):
            got[i, way, 1] = go(hop(i, way, 1), zcopies)
    go(cross(1, z, 0, None), ycopies)
    count = 2

    def onward(i, h):
        nonlocal count
        for way in (0, 1):
            got[i, way, h].wait_recv()
            if h < far:
                got[i, way, h + 1] = go(hop(i, way, h + 1), zcopies)
            if i == 0:
                sign = 1 - 2 * way
                go(cross(count, zof(-sign * h), 0, way if h == far else None), ycopies)
                count += 1

    onward(0, 1)
    second.wait_recv()
    for way in (0, 1):
        got[2, way, 1] = go(hop(2, way, 1), zcopies)
    onward(1, 1)
    for h in range(2, far + 1):
        onward(0, h)
        onward(2, h - 1)
        onward(1, h)
    onward(2, far)
    for copy in ycopies[1:]:
        copy.wait_recv()
    for copy in [*ycopies, *zcopies]:
        copy.wait_send()
    for j in range(1, tasks):
        c_remote(j).wait_send()

    def sent(copies):
        for copy in copies:
            copy.wait_send()

    def close_a(u):
        sent(ya(u))
        for m, sign, _, _ in messages(u):
            sent(za(u, m, sign))

    def close_b(u):
        sent(yb(u))
        for m, sign, _, _ in messages(u):
            sent(zb(u, m, sign))
    each(sum(first_y), close_a)
    each(sum(first_z), close_b)


def solution(mesh):
    tasks, ndp = mesh.shape["task"], mesh.shape["dp"]
    nz = ndp // 2

    def on_device(inputs, cotangent, task_order, conflict_flags):
        cot = cotangent[0]
        tokens = cot.shape[0]
        rows = inputs.shape[1] // ndp
        step = min(rows, 128)
        blocks = rows // step
        width = cot.shape[1] // tasks
        na = sum(plan(tasks, blocks))
        nb = tasks * blocks - na
        vmem, dma = pltpu.VMEM, pltpu.SemaphoreType.DMA
        f32, i16, bf16 = jnp.float32, jnp.int16, jnp.bfloat16
        hops = max(nz - 1, 1)
        scratch = [
            vmem(inputs.shape, bf16), vmem((ndp * blocks, step, tokens), bf16), vmem((tasks, tokens, width), bf16),
            vmem((na, nz, step, width), i16), vmem((na, nz, 1, width), f32),
            vmem((na, nz, step, width), i16), vmem((na, nz, 1, width), f32),
            vmem((na, hops, step, width), i16), vmem((na, hops, 1, width), f32),
            vmem((na, hops, step, width), i16), vmem((na, hops, 1, width), f32),
            vmem((na, nz, step, width), f32),
            vmem((nb, step, width), i16), vmem((nb, 1, width), f32),
            vmem((nb, step, width), i16), vmem((nb, 1, width), f32),
            vmem((nb, hops, 2, step, width), i16), vmem((nb, hops, 2, 1, width), f32),
            vmem((nb, hops, 2, step, width), i16), vmem((nb, hops, 2, 1, width), f32),
            vmem((nb, 2, step, width), f32),
            vmem((tasks, blocks, step, width), f32),
            vmem((8, 128), f32), vmem((ndp, 8, 128), f32), vmem((8, 128), f32), vmem((tasks, 8, 128), f32),
            dma((ndp,)), dma, dma((tasks,)), dma((tasks,)),
            dma((na, 2)), dma((na, 2)), dma((na, hops, 2)), dma((na, hops, 2)),
            dma((nb, 2)), dma((nb, 2)), dma((nb, hops, 2)), dma((nb, hops, 2)),
            dma((ndp,)), dma((ndp,)), dma((tasks,)), dma((tasks,)),
            dma((3, 2, nz)), dma((3, 2, nz)), dma((nz + 2,)), dma((nz + 2,)),
        ]
        smem = pl.BlockSpec(memory_space=pltpu.SMEM)
        whole = pl.BlockSpec(memory_space=pltpu.VMEM)
        hbm = pl.BlockSpec(memory_space=pl.ANY)
        return pl.pallas_call(
            functools.partial(kernel, tasks, ndp, blocks),
            out_shape=jax.ShapeDtypeStruct((inputs.shape[1], width), jnp.bfloat16),
            in_specs=[smem, smem, hbm, hbm],
            out_specs=whole,
            scratch_shapes=scratch,
            compiler_params=pltpu.CompilerParams(collective_id=0, has_side_effects=True,
                                                 vmem_limit_bytes=60 * 1024 * 1024),
        )(task_order, conflict_flags, inputs, cot)

    return jax.shard_map(
        on_device, mesh=mesh,
        in_specs=(P("dp", None), P("task", "dp", None), P(), P()),
        out_specs=P(None, "task"), check_vma=False,
    )
```

time: 169 us -> 162 us (0.959); the launches traced: 167 us -> 162 us
  Pallas kernels: 163 us -> 159 us
    pallas_call x1, Pallas kernels: 163 us -> 159 us  [on_device(): pl.pallas_call(functools.partial(kernel, tasks, ndp, blocks), out_shape=j...]
where the time goes in v1:
time: 162 us
  Pallas kernels  159 us (98%)
  local copies, waits for them, and re-layouts  3.05 us (2%)
    pallas_call x1, Pallas kernels, on_device(): pl.pallas_call(functools.partial(kernel, tasks, ndp, blocks), out_shape=j...  159 us

profile of v1, /device:TPU:0, one launch (start us, length us, event | category | flops | bytes accessed | tf_op | source)
XLA Modules:
  0.0 162.1 jit_solution(11895700535916458389)
XLA Ops:
  0.0 159.1 %shard_map.46 = bf16[4096,256]{1,0:T(8,128)(2,1)} custom-call(s32[4]{0:T(128)} %order_ref.1, s32[4,4]{1,0:T(4,128)} %flags_ref.1, bf16[1024,4096]{1,0:T(8,128)(2,1)} %x_hbm.1, bf16[1024,1024]{1,0:T(8,128)(2,1)} %bitcast.1), custom_call_target="tpu_custom_call" | custom-call | tf_op jit(solution)/shard_map/pallas_call | solution.py:465
  159.1 3.0 %copy.6 = bf16[4096,256]{1,0:T(8,128)(2,1)} copy(bf16[4096,256]{1,0:T(8,128)(2,1)} %shard_map.46) | data formatting | bytes 4194304

commit v2 on v0

v2 whole, which is shorter than its diff:
```python
import functools

import jax
import jax.numpy as jnp
from jax import lax
from jax.experimental import pallas as pl
from jax.experimental.pallas import tpu as pltpu
from jax.sharding import PartitionSpec as P

MESH = pl.DeviceIdType.MESH
TOP = 32767.0
LAG = 3
PIECES = 8
CROSSING = 6


def coded(tile):
    high = jnp.maximum(jnp.max(jnp.abs(tile), axis=0, keepdims=True), 1e-30)
    code = jnp.round(tile * (TOP / high)).astype(jnp.int32).astype(jnp.int16)
    return code, high * (1.0 / TOP)


def decoded(code, scale):
    return code.astype(jnp.int32).astype(jnp.float32) * scale


def shares(blocks):
    low = blocks * 7 // 16
    return low, blocks * 7 // 8 - low


def kernel(tasks, ndp, blocks, order_ref, flags_ref, x_hbm, c_hbm, out_ref,
           x_ref, cots, acc, ysend_a, yscale_a, yrecv_a, yrscale_a, zsend_a, zscale_a, zrecv_a, zrscale_a,
           ysend_b, yscale_b, yrecv_b, yrscale_b, zsend_b, zscale_b, zrecv_b, zrscale_b,
           grads, gram_own, gram_dp, gram_mid, gram_task,
           x_sem, c_sem, cs_sem, cr_sem,
           yas_sem, yar_sem, zas_sem, zar_sem, ybs_sem, ybr_sem, zbs_sem, zbr_sem,
           gs_sem, gr_sem, hs_sem, hr_sem, zgs_sem, zgr_sem, ygs_sem, ygr_sem, yhs_sem, yhr_sem):
    nz = ndp // 2
    pairs_of = tasks // 2
    me_t = lax.axis_index("task")
    me_d = lax.axis_index("dp")
    z = me_d // 2
    y = me_d % 2
    step = acc.shape[1]
    width = cots.shape[2]
    rows = step * blocks
    low_b, high_b = shares(blocks)
    low_a, high_a = blocks - high_b, blocks - low_b
    pair_b, pair_a = low_b + high_b, low_a + high_a
    units_a, units_b = pair_a * pairs_of, pair_b * pairs_of
    at_end = (z == 0) | (z == nz - 1)

    def dp_at(zi, yi):
        return zi * 2 + yi

    def mate(j, way):
        return lax.rem(me_t // 2 + way * (j // 2) + pairs_of, pairs_of) * 2 + lax.rem(me_t % 2 + j % 2, 2)

    def place_a(u):
        r = u % pair_a
        return u // pair_a * 2 + r // high_a, r % high_a

    def place_b(u):
        r = u % pair_b
        odd = (r + high_b - low_b) // high_b
        return u // pair_b * 2 + odd, r - odd * low_b + high_a - odd * (high_a - low_a)

    partner = (me_t, dp_at(z, 1 - y))

    def remote(src, dst, s, r, device):
        return pltpu.make_async_remote_copy(src_ref=src, dst_ref=dst, send_sem=s, recv_sem=r,
                                            device_id=device, device_id_type=MESH)

    c_copy = pltpu.make_async_copy(c_hbm.at[:, pl.ds(pl.multiple_of(me_t * width, width), width)], cots.at[0], c_sem)
    c_copy.start()
    x_copies = []
    for d in range(4):
        part = pl.ds(d * rows, rows)
        x_copies.append(pltpu.make_async_copy(x_hbm.at[:, part], x_ref.at[:, part], x_sem.at[d]))
        x_copies[-1].start()

    barrier = pltpu.get_barrier_semaphore()
    for k in range(1, ndp):
        pl.semaphore_signal(barrier, inc=1, device_id=(me_t, lax.rem(me_d + k, ndp)), device_id_type=MESH)
    for k in range(1, tasks):
        pl.semaphore_signal(barrier, inc=1, device_id=(lax.rem(me_t + k, tasks), me_d), device_id_type=MESH)
    pl.semaphore_wait(barrier, ndp + tasks - 2)

    def c_remote(j):
        peer = mate(j, 1)
        return remote(c_hbm.at[:, pl.ds(pl.multiple_of(peer * width, width), width)], cots.at[j],
                      cs_sem.at[j], cr_sem.at[j], (peer, me_d))

    for j in range(1, tasks):
        c_remote(j).start()
    c_copy.wait()
    for copy in x_copies:
        copy.wait()

    def product(j, block, end, yi):
        first = pl.multiple_of((dp_at(end, yi) * blocks + block) * step, step)
        return lax.dot_general(x_ref[:, pl.ds(first, step)], cots[j], (((0,), (0,)), ((), ())),
                               preferred_element_type=jnp.float32)

    def hop(end):
        return z if end else nz - 1 - z

    def ahead(end):
        return (me_t, dp_at(jnp.clip(z + (1 if end else -1), 0, nz - 1), y))

    def ya(u, end):
        return (remote(ysend_a.at[u, end], yrecv_a.at[u, end], yas_sem.at[u, end, 0], yar_sem.at[u, end, 0], partner),
                remote(yscale_a.at[u, end], yrscale_a.at[u, end], yas_sem.at[u, end, 1], yar_sem.at[u, end, 1], partner))

    def yb(u):
        return (remote(ysend_b.at[u], yrecv_b.at[u], ybs_sem.at[u, 0], ybr_sem.at[u, 0], partner),
                remote(yscale_b.at[u], yrscale_b.at[u], ybs_sem.at[u, 1], ybr_sem.at[u, 1], partner))

    def za(u, end):
        device = ahead(end)
        return (remote(zsend_a.at[u, end], zrecv_a.at[u, end], zas_sem.at[u, end, 0], zar_sem.at[u, end, 0], device),
                remote(zscale_a.at[u, end], zrscale_a.at[u, end], zas_sem.at[u, end, 1], zar_sem.at[u, end, 1], device))

    def zb(i, end):
        device = ahead(end)
        return (remote(zsend_b.at[i, end], zrecv_b.at[i, end], zbs_sem.at[i, end, 0], zbr_sem.at[i, end, 0], device),
                remote(zscale_b.at[i, end], zrscale_b.at[i, end], zbs_sem.at[i, end, 1], zbr_sem.at[i, end, 1], device))

    def start(copies):
        for copy in copies:
            copy.start()

    def arrive(copies):
        for copy in copies:
            copy.wait_recv()

    def each(first, last, body):
        if last > first:
            lax.fori_loop(first, last, lambda i, carry: (body(i), carry)[1], 0)

    def a_y(j, i):
        u = j // 2 * pair_a + j % 2 * high_a + i
        for end in (0, 1):
            code, scale = coded(product(j, i, end, 1 - y))
            ysend_a[u, end] = code
            yscale_a[u, end] = scale
            start(ya(u, end))

    def b_z(i, end):
        u, p = i // 2, i % 2
        j, block = place_b(u)
        acc[end] = product(j, block, end, lax.rem(1 - y + p, 2))

        @pl.when(hop(end) > 0)
        def _():
            arrive(zb(i, end))
            acc[end] = acc[end] + decoded(zrecv_b[i, end], zrscale_b[i, end])

        @pl.when(hop(end) < nz - 1)
        def _():
            code, scale = coded(acc[end])
            zsend_b[i, end] = code
            zscale_b[i, end] = scale
            start(zb(i, end))

        @pl.when((hop(end) == nz - 1) & (p == 0))
        def _():
            code, scale = coded(acc[end])
            ysend_b[u] = code
            yscale_b[u] = scale
            start(yb(u))

        @pl.when((hop(end) == nz - 1) & (p == 1))
        def _():
            grads[mate(j, -1), block] = acc[end]

    def a_z(u, end):
        j, block = place_a(u)
        total = product(j, block, end, y)
        arrive(ya(u, end))
        acc[end] = total + decoded(yrecv_a[u, end], yrscale_a[u, end])

        @pl.when(hop(end) > 0)
        def _():
            arrive(za(u, end))
            acc[end] = acc[end] + decoded(zrecv_a[u, end], zrscale_a[u, end])

        @pl.when(hop(end) < nz - 1)
        def _():
            code, scale = coded(acc[end])
            zsend_a[u, end] = code
            zscale_a[u, end] = scale
            start(za(u, end))

        @pl.when(hop(end) == nz - 1)
        def _():
            grads[mate(j, -1), block] = acc[end]

    items_b = 2 * units_b

    def advance(s):
        for end in (1, 0):
            at = s - LAG * hop(end)

            @pl.when((at >= 0) & (at < items_b))
            def _():
                b_z(at, end)

            @pl.when((at >= items_b) & (at < items_b + units_a))
            def _():
                a_z(at - items_b, end)

    s = 0
    for j in range(tasks):
        if j:
            c_remote(j).wait_recv()
        steps = 2 * (high_b if j % 2 else low_b)
        count = low_a if j % 2 else high_a
        several = -(-count // steps)

        def both(i, first=s, j=j, count=count, several=several):
            for q in range(several):
                @pl.when((i - first) * several + q < count)
                def _():
                    a_y(j, (i - first) * several + q)
            advance(i)
        each(s, s + steps, both)
        s += steps
    each(s, items_b + units_a + LAG * (nz - 1), advance)

    def finish_b(u):
        j, block = place_b(u)
        arrive(yb(u))
        task = mate(j, -1)
        grads[task, block] = grads[task, block] + decoded(yrecv_b[u], yrscale_b[u])

    end_of = z // max(nz - 1, 1)
    mine = dp_at(end_of, y) * rows

    def weigh():
        each(0, units_b, finish_b)
        pairs = [(s, t) for s in range(tasks) for t in range(s, tasks)]

        def products(index, sums):
            held = [grads[t, index] for t in range(tasks)]
            return tuple(total + jnp.sum((held[s] * held[t]).reshape(step // 8, 8, width), axis=0)
                         for total, (s, t) in zip(sums, pairs))

        sums = lax.fori_loop(0, blocks, products, tuple(jnp.zeros((8, width), jnp.float32) for _ in pairs))
        line = lax.broadcasted_iota(jnp.int32, (8, 128), 0)
        lane = lax.broadcasted_iota(jnp.int32, (8, 128), 1)
        gram = jnp.zeros((8, 128), jnp.float32)
        for total, (s, t) in zip(sums, pairs):
            value = jnp.sum(jnp.sum(total, axis=0, keepdims=True), axis=1, keepdims=True)
            here = ((line == s) & (lane == t)) | ((line == t) & (lane == s))
            gram = gram + jnp.where(here, value, 0.0)

        def swap(value, buffer_own, buffer, count, s_sem, r_sem, device):
            buffer_own[...] = value
            copies = [remote(buffer_own, buffer.at[k], s_sem.at[k], r_sem.at[k], device(k)) for k in range(1, count)]
            start(copies)
            for k, copy in enumerate(copies, 1):
                copy.wait_recv()
                value = value + buffer[k]
            for copy in copies:
                copy.wait_send()
            return value

        def other(k):
            return (me_t, dp_at(z if k % 2 == k else nz - 1 - z, y if k % 2 == 0 else 1 - y))

        gram = swap(gram, gram_own, gram_dp, 4, gs_sem, gr_sem, other)
        gram = swap(gram, gram_mid, gram_task, tasks, hs_sem, hr_sem, lambda k: (lax.rem(me_t + k, tasks), me_d))

        cols = [jnp.sum(jnp.where(lane == m, gram, 0.0), axis=1, keepdims=True) for m in range(tasks)]
        entry = lambda column, i: jnp.sum(jnp.where(line[:, :1] == i, column, 0.0), axis=0, keepdims=True)
        row = line[:, :1]
        coefficients = [(row == m).astype(jnp.float32) for m in range(tasks)]
        flag_cols = []
        for m in range(tasks):
            column = jnp.zeros((8, 1), jnp.float32)
            for i in range(tasks):
                column = column + jnp.where(row == i, flags_ref[i, m].astype(jnp.float32), 0.0)
            flag_cols.append(column)
        for position in range(tasks):
            target = order_ref[position]
            picks = [jnp.where(target == m, 1.0, 0.0) for m in range(tasks)]
            column = sum(cols[m] * picks[m] for m in range(tasks))
            dots = sum(coefficients[m] * entry(column, m) for m in range(tasks))
            square = sum(entry(column, m) * picks[m] for m in range(tasks))
            active = sum(flag_cols[m] * picks[m] for m in range(tasks)) * jnp.where(row == target, 0.0, 1.0)
            removed = jnp.minimum(dots, 0.0) / square * active
            coefficients = [coefficients[m] - removed * picks[m] for m in range(tasks)]
        weights = [jnp.sum(coefficients[m], axis=0, keepdims=True) for m in range(tasks)]

        def mix(index, carry):
            mixed = sum(weights[t] * grads[t, index] for t in range(tasks))
            out_ref[pl.ds(pl.multiple_of(mine + index * step, step), step), :] = mixed.astype(jnp.bfloat16)
            return carry
        lax.fori_loop(0, blocks, mix, 0)

    pl.when(at_end)(weigh)

    size = rows // PIECES
    chunks = 2 * PIECES - CROSSING

    def segment(end, yi, chunk):
        return out_ref.at[pl.ds(pl.multiple_of(dp_at(end, yi) * rows + chunk * size, size), size), :]

    def along(end, i):
        chunk = jnp.where(i < PIECES, i, i - PIECES + CROSSING)
        ref = segment(end, jnp.where(i < PIECES, y, 1 - y), chunk)
        return remote(ref, ref, zgs_sem.at[end, i], zgr_sem.at[end, i], ahead(1 - end))

    def over(end, i):
        ref = segment(end, y, i)
        return remote(ref, ref, ygs_sem.at[end, i], ygr_sem.at[end, i], partner)

    def early(i):
        ref = segment(end_of, y, i)
        return remote(ref, ref, yhs_sem.at[i], yhr_sem.at[i], partner)

    @pl.when(at_end)
    def _():
        each(CROSSING, PIECES, lambda i: early(i).start())

    def spread(s):
        for end in (0, 1):
            far = hop(1 - end)
            i = s - LAG * far

            @pl.when((i >= 0) & (i < chunks))
            def _():
                @pl.when(far > 0)
                def _():
                    along(end, i).wait_recv()

                @pl.when((far == 0) & (i >= PIECES))
                def _():
                    early(i - PIECES + CROSSING).wait_recv()

                @pl.when(far < nz - 1)
                def _():
                    along(end, i).start()

                @pl.when(i < CROSSING)
                def _():
                    over(end, i).start()

    each(0, chunks + LAG * (nz - 1), spread)

    def close(i):
        for end in (0, 1):
            over(end, i).wait_recv()
            over(end, i).wait_send()
    each(0, CROSSING, close)

    @pl.when(at_end)
    def _():
        each(CROSSING, PIECES, lambda i: early(i).wait_send())

    for j in range(1, tasks):
        c_remote(j).wait_send()

    def sent(copies):
        for copy in copies:
            copy.wait_send()

    def close_y(u):
        for end in (0, 1):
            sent(ya(u, end))
    each(0, units_a, close_y)
    pl.when(at_end)(lambda: each(0, units_b, lambda u: sent(yb(u))))
    for end in (0, 1):
        @pl.when(hop(end) < nz - 1)
        def _():
            each(0, units_a, lambda u: sent(za(u, end)))
            each(0, items_b, lambda i: sent(zb(i, end)))
            each(0, chunks, lambda i: along(1 - end, i).wait_send())


def solution(mesh):
    tasks, ndp = mesh.shape["task"], mesh.shape["dp"]

    def on_device(inputs, cotangent, task_order, conflict_flags):
        cot = cotangent[0]
        tokens = cot.shape[0]
        rows = inputs.shape[1] // 4
        step = min(rows, 128)
        blocks = rows // step
        width = cot.shape[1] // tasks
        nb = sum(shares(blocks)) * (tasks // 2)
        na = tasks * blocks - nb
        vmem, dma = pltpu.VMEM, pltpu.SemaphoreType.DMA
        f32, i16, bf16 = jnp.float32, jnp.int16, jnp.bfloat16
        code, scale = (step, width), (1, width)
        chunks = 2 * PIECES - CROSSING
        scratch = [
            vmem(inputs.shape, bf16), vmem((tasks, tokens, width), bf16), vmem((2, step, width), f32),
            vmem((na, 2, *code), i16), vmem((na, 2, *scale), f32), vmem((na, 2, *code), i16), vmem((na, 2, *scale), f32),
            vmem((na, 2, *code), i16), vmem((na, 2, *scale), f32), vmem((na, 2, *code), i16), vmem((na, 2, *scale), f32),
            vmem((nb, *code), i16), vmem((nb, *scale), f32), vmem((nb, *code), i16), vmem((nb, *scale), f32),
            vmem((2 * nb, 2, *code), i16), vmem((2 * nb, 2, *scale), f32),
            vmem((2 * nb, 2, *code), i16), vmem((2 * nb, 2, *scale), f32),
            vmem((tasks, blocks, step, width), f32),
            vmem((8, 128), f32), vmem((4, 8, 128), f32), vmem((8, 128), f32), vmem((tasks, 8, 128), f32),
            dma((4,)), dma, dma((tasks,)), dma((tasks,)),
            dma((na, 2, 2)), dma((na, 2, 2)), dma((na, 2, 2)), dma((na, 2, 2)),
            dma((nb, 2)), dma((nb, 2)), dma((2 * nb, 2, 2)), dma((2 * nb, 2, 2)),
            dma((4,)), dma((4,)), dma((tasks,)), dma((tasks,)),
            dma((2, chunks)), dma((2, chunks)), dma((2, CROSSING)), dma((2, CROSSING)), dma((PIECES,)), dma((PIECES,)),
        ]
        smem = pl.BlockSpec(memory_space=pltpu.SMEM)
        whole = pl.BlockSpec(memory_space=pltpu.VMEM)
        hbm = pl.BlockSpec(memory_space=pl.ANY)
        return pl.pallas_call(
            functools.partial(kernel, tasks, ndp, blocks),
            out_shape=jax.ShapeDtypeStruct((inputs.shape[1], width), jnp.bfloat16),
            in_specs=[smem, smem, hbm, hbm],
            out_specs=whole,
            scratch_shapes=scratch,
            compiler_params=pltpu.CompilerParams(collective_id=0, has_side_effects=True,
                                                 vmem_limit_bytes=60 * 1024 * 1024),
        )(task_order, conflict_flags, inputs, cot)

    return jax.shard_map(
        on_device, mesh=mesh,
        in_specs=(P("dp", None), P("task", "dp", None), P(), P()),
        out_specs=P(None, "task"), check_vma=False,
    )
```

time: 169 us -> 129 us (0.76); the launches traced: 167 us -> 129 us
  Pallas kernels: 163 us -> 126 us
    pallas_call x1, Pallas kernels: 163 us -> 126 us  [on_device(): pl.pallas_call(functools.partial(kernel, tasks, ndp, blocks), out_shape=j...]
where the time goes in v2:
time: 129 us
  Pallas kernels  126 us (98%)
  local copies, waits for them, and re-layouts  3.05 us (2%)
    pallas_call x1, Pallas kernels, on_device(): pl.pallas_call(functools.partial(kernel, tasks, ndp, blocks), out_shape=j...  126 us
    unnamed x1, local copies, waits for them, and re-layouts  3.05 us

profile of v2, /device:TPU:0, one launch (start us, length us, event | category | flops | bytes accessed | tf_op | source)
XLA Modules:
  0.0 128.9 jit_solution(5630430521992519360)
XLA Ops:
  0.0 125.8 %shard_map.46 = bf16[4096,256]{1,0:T(8,128)(2,1)} custom-call(s32[4]{0:T(128)} %order_ref.1, s32[4,4]{1,0:T(4,128)} %flags_ref.1, bf16[1024,4096]{1,0:T(8,128)(2,1)} %x_hbm.1, bf16[1024,1024]{1,0:T(8,128)(2,1)} %bitcast.1), custom_call_target="tpu_custom_call" | custom-call | tf_op jit(solution)/shard_map/pallas_call | solution.py:417
  125.9 3.0 %copy.6 = bf16[4096,256]{1,0:T(8,128)(2,1)} copy(bf16[4096,256]{1,0:T(8,128)(2,1)} %shard_map.46) | data formatting | bytes 4194304

commit v3 on v2

--- a/solution.py
+++ b/solution.py
@@ -10,8 +10,10 @@
 MESH = pl.DeviceIdType.MESH
 TOP = 32767.0
 LAG = 3
-PIECES = 8
-CROSSING = 6
+SHARE = 12
+REACH = 5
+PIECES = 16
+CROSSING = 12
 
 
 def coded(tile):
@@ -25,17 +27,17 @@
 
 
 def shares(blocks):
-    low = blocks * 7 // 16
-    return low, blocks * 7 // 8 - low
+    low = blocks * SHARE // 32
+    return low, blocks * SHARE // 16 - low
 
 
 def kernel(tasks, ndp, blocks, order_ref, flags_ref, x_hbm, c_hbm, out_ref,
            x_ref, cots, acc, ysend_a, yscale_a, yrecv_a, yrscale_a, zsend_a, zscale_a, zrecv_a, zrscale_a,
            ysend_b, yscale_b, yrecv_b, yrscale_b, zsend_b, zscale_b, zrecv_b, zrscale_b,
-           grads, gram_own, gram_dp, gram_mid, gram_task,
+           grads, gram_own, gram_all,
            x_sem, c_sem, cs_sem, cr_sem,
            yas_sem, yar_sem, zas_sem, zar_sem, ybs_sem, ybr_sem, zbs_sem, zbr_sem,
-           gs_sem, gr_sem, hs_sem, hr_sem, zgs_sem, zgr_sem, ygs_sem, ygr_sem, yhs_sem, yhr_sem):
+           gs_sem, gr_sem, zgs_sem, zgr_sem, ygs_sem, ygr_sem, yhs_sem, yhr_sem):
     nz = ndp // 2
     pairs_of = tasks // 2
     me_t = lax.axis_index("task")
@@ -80,12 +82,21 @@
         x_copies.append(pltpu.make_async_copy(x_hbm.at[:, part], x_ref.at[:, part], x_sem.at[d]))
         x_copies[-1].start()
 
+    def hop(end):
+        return z if end else nz - 1 - z
+
+    def ahead(end):
+        return (me_t, dp_at(jnp.clip(z + (1 if end else -1), 0, nz - 1), y))
+
     barrier = pltpu.get_barrier_semaphore()
-    for k in range(1, ndp):
-        pl.semaphore_signal(barrier, inc=1, device_id=(me_t, lax.rem(me_d + k, ndp)), device_id_type=MESH)
+    pl.semaphore_signal(barrier, inc=1, device_id=partner, device_id_type=MESH)
     for k in range(1, tasks):
         pl.semaphore_signal(barrier, inc=1, device_id=(lax.rem(me_t + k, tasks), me_d), device_id_type=MESH)
-    pl.semaphore_wait(barrier, ndp + tasks - 2)
+    for end in (0, 1):
+        @pl.when(hop(end) < nz - 1)
+        def _():
+            pl.semaphore_signal(barrier, inc=1, device_id=ahead(end), device_id_type=MESH)
+    pl.semaphore_wait(barrier, tasks + jnp.where(z > 0, 1, 0) + jnp.where(z < nz - 1, 1, 0))
 
     def c_remote(j):
         peer = mate(j, 1)
@@ -102,12 +113,6 @@
         first = pl.multiple_of((dp_at(end, yi) * blocks + block) * step, step)
         return lax.dot_general(x_ref[:, pl.ds(first, step)], cots[j], (((0,), (0,)), ((), ())),
                                preferred_element_type=jnp.float32)
-
-    def hop(end):
-        return z if end else nz - 1 - z
-
-    def ahead(end):
-        return (me_t, dp_at(jnp.clip(z + (1 if end else -1), 0, nz - 1), y))
 
     def ya(u, end):
         return (remote(ysend_a.at[u, end], yrecv_a.at[u, end], yas_sem.at[u, end, 0], yar_sem.at[u, end, 0], partner),
@@ -169,7 +174,10 @@
             code, scale = coded(acc[end])
             ysend_b[u] = code
             yscale_b[u] = scale
-            start(yb(u))
+
+            @pl.when(i >= held)
+            def _():
+                start(yb(u))
 
         @pl.when((hop(end) == nz - 1) & (p == 1))
         def _():
@@ -198,6 +206,7 @@
             grads[mate(j, -1), block] = acc[end]
 
     items_b = 2 * units_b
+    held = max(items_b - LAG * (nz - 1), 0)
 
     def advance(s):
         for end in (1, 0):
@@ -227,6 +236,7 @@
             advance(i)
         each(s, s + steps, both)
         s += steps
+    pl.when(at_end)(lambda: each(0, -(-held // 2), lambda u: start(yb(u))))
     each(s, items_b + units_a + LAG * (nz - 1), advance)
 
     def finish_b(u):
@@ -256,22 +266,18 @@
             here = ((line == s) & (lane == t)) | ((line == t) & (lane == s))
             gram = gram + jnp.where(here, value, 0.0)
 
-        def swap(value, buffer_own, buffer, count, s_sem, r_sem, device):
-            buffer_own[...] = value
-            copies = [remote(buffer_own, buffer.at[k], s_sem.at[k], r_sem.at[k], device(k)) for k in range(1, count)]
-            start(copies)
-            for k, copy in enumerate(copies, 1):
-                copy.wait_recv()
-                value = value + buffer[k]
-            for copy in copies:
-                copy.wait_send()
-            return value
-
-        def other(k):
-            return (me_t, dp_at(z if k % 2 == k else nz - 1 - z, y if k % 2 == 0 else 1 - y))
-
-        gram = swap(gram, gram_own, gram_dp, 4, gs_sem, gr_sem, other)
-        gram = swap(gram, gram_mid, gram_task, tasks, hs_sem, hr_sem, lambda k: (lax.rem(me_t + k, tasks), me_d))
+        def peer(k):
+            end = k // 2 % 2
+            return (lax.rem(me_t + k // 4, tasks), dp_at(nz - 1 - z if end else z, 1 - y if k % 2 else y))
+
+        gram_own[...] = gram
+        copies = [remote(gram_own, gram_all.at[k], gs_sem.at[k], gr_sem.at[k], peer(k)) for k in range(1, 4 * tasks)]
+        start(copies)
+        for k, copy in enumerate(copies, 1):
+            copy.wait_recv()
+            gram = gram + gram_all[k]
+        for copy in copies:
+            copy.wait_send()
 
         cols = [jnp.sum(jnp.where(lane == m, gram, 0.0), axis=1, keepdims=True) for m in range(tasks)]
         entry = lambda column, i: jnp.sum(jnp.where(line[:, :1] == i, column, 0.0), axis=0, keepdims=True)
@@ -328,7 +334,7 @@
     def spread(s):
         for end in (0, 1):
             far = hop(1 - end)
-            i = s - LAG * far
+            i = s - REACH * far
 
             @pl.when((i >= 0) & (i < chunks))
             def _():
@@ -348,7 +354,7 @@
                 def _():
                     over(end, i).start()
 
-    each(0, chunks + LAG * (nz - 1), spread)
+    each(0, chunks + REACH * (nz - 1), spread)
 
     def close(i):
         for end in (0, 1):
@@ -404,16 +410,16 @@
             vmem((2 * nb, 2, *code), i16), vmem((2 * nb, 2, *scale), f32),
             vmem((2 * nb, 2, *code), i16), vmem((2 * nb, 2, *scale), f32),
             vmem((tasks, blocks, step, width), f32),
-            vmem((8, 128), f32), vmem((4, 8, 128), f32), vmem((8, 128), f32), vmem((tasks, 8, 128), f32),
+            vmem((8, 128), f32), vmem((4 * tasks, 8, 128), f32),
             dma((4,)), dma, dma((tasks,)), dma((tasks,)),
             dma((na, 2, 2)), dma((na, 2, 2)), dma((na, 2, 2)), dma((na, 2, 2)),
             dma((nb, 2)), dma((nb, 2)), dma((2 * nb, 2, 2)), dma((2 * nb, 2, 2)),
-            dma((4,)), dma((4,)), dma((tasks,)), dma((tasks,)),
+            dma((4 * tasks,)), dma((4 * tasks,)),
             dma((2, chunks)), dma((2, chunks)), dma((2, CROSSING)), dma((2, CROSSING)), dma((PIECES,)), dma((PIECES,)),
         ]
         smem = pl.BlockSpec(memory_space=pltpu.SMEM)
         whole = pl.BlockSpec(memory_space=pltpu.VMEM)
-        hbm = pl.BlockSpec(memory_space=pl.ANY)
+        hbm = pl.BlockSpec(memory_space=pltpu.HBM)
         return pl.pallas_call(
             functools.partial(kernel, tasks, ndp, blocks),
             out_shape=jax.ShapeDtypeStruct((inputs.shape[1], width), jnp.bfloat16),
@@ -421,8 +427,8 @@
             out_specs=whole,
             scratch_shapes=scratch,
             compiler_params=pltpu.CompilerParams(collective_id=0, has_side_effects=True,
-                                                 vmem_limit_bytes=60 * 1024 * 1024),
-        )(task_order, conflict_flags, inputs, cot)
+                                                 vmem_limit_bytes=44 * 1024 * 1024),
+        )(*[pltpu.with_memory_space_constraint(v, pltpu.HBM) for v in (task_order, conflict_flags, inputs, cot)])
 
     return jax.shard_map(
         on_device, mesh=mesh,

time: 129 us -> 122 us (0.946)
  Pallas kernels: 126 us -> 120 us
  local copies, waits for them, and re-layouts: 3.05 us -> 1.32 us
    pallas_call x1, Pallas kernels: 126 us -> 120 us  [on_device(): pl.pallas_call(functools.partial(kernel, tasks, ndp, blocks), out_shape=j...]
    unnamed x1, local copies, waits for them, and re-layouts: 3.05 us -> 1.32 us
where the time goes in v3:
time: 122 us
  Pallas kernels  120 us (98%)
  local copies, waits for them, and re-layouts  1.32 us (1%)
    pallas_call x1, Pallas kernels, on_device(): pl.pallas_call(functools.partial(kernel, tasks, ndp, blocks), out_shape=j...  120 us

profile of v3, /device:TPU:0, one launch (start us, length us, event | category | flops | bytes accessed | tf_op | source)
XLA Modules:
  0.0 121.7 jit_solution(296256564881107836)
XLA Ops:
  0.0 120.4 %shard_map.46 = bf16[4096,256]{1,0:T(8,128)(2,1)S(1)} custom-call(s32[4]{0:T(128)} %order_ref.1, s32[4,4]{1,0:T(4,128)} %flags_ref.1, bf16[1024,4096]{1,0:T(8,128)(2,1)} %x_hbm.1, bf16[1024,1024]{1,0:T(8,128)(2,1)} %bitcast.1), custom_call_target="tpu_custom_call" | custom-call | tf_op jit(solution)/shard_map/pallas_call | solution.py:423
  120.4 1.3 %copy.6 = bf16[4096,256]{1,0:T(8,128)(2,1)} copy(bf16[4096,256]{1,0:T(8,128)(2,1)S(1)} %shard_map.46) | data formatting | bytes 4194304

commit v4 on v3

--- a/solution.py
+++ b/solution.py
@@ -78,7 +78,7 @@
     c_copy.start()
     x_copies = []
     for d in range(4):
-        part = pl.ds(d * rows, rows)
+        part = pl.ds(pl.multiple_of(dp_at(d % 2, 1 - y if d < 2 else y) * rows, rows), rows)
         x_copies.append(pltpu.make_async_copy(x_hbm.at[:, part], x_ref.at[:, part], x_sem.at[d]))
         x_copies[-1].start()
 
@@ -106,7 +106,7 @@
     for j in range(1, tasks):
         c_remote(j).start()
     c_copy.wait()
-    for copy in x_copies:
+    for copy in x_copies[:2]:
         copy.wait()
 
     def product(j, block, end, yi):
@@ -114,9 +114,9 @@
         return lax.dot_general(x_ref[:, pl.ds(first, step)], cots[j], (((0,), (0,)), ((), ())),
                                preferred_element_type=jnp.float32)
 
-    def ya(u, end):
-        return (remote(ysend_a.at[u, end], yrecv_a.at[u, end], yas_sem.at[u, end, 0], yar_sem.at[u, end, 0], partner),
-                remote(yscale_a.at[u, end], yrscale_a.at[u, end], yas_sem.at[u, end, 1], yar_sem.at[u, end, 1], partner))
+    def ya(u):
+        return (remote(ysend_a.at[u], yrecv_a.at[u], yas_sem.at[u, 0], yar_sem.at[u, 0], partner),
+                remote(yscale_a.at[u], yrscale_a.at[u], yas_sem.at[u, 1], yar_sem.at[u, 1], partner))
 
     def yb(u):
         return (remote(ysend_b.at[u], yrecv_b.at[u], ybs_sem.at[u, 0], ybr_sem.at[u, 0], partner),
@@ -150,7 +150,7 @@
             code, scale = coded(product(j, i, end, 1 - y))
             ysend_a[u, end] = code
             yscale_a[u, end] = scale
-            start(ya(u, end))
+        start(ya(u))
 
     def b_z(i, end):
         u, p = i // 2, i % 2
@@ -185,9 +185,12 @@
 
     def a_z(u, end):
         j, block = place_a(u)
-        total = product(j, block, end, y)
-        arrive(ya(u, end))
-        acc[end] = total + decoded(yrecv_a[u, end], yrscale_a[u, end])
+        acc[end] = product(j, block, end, y)
+
+        @pl.when(hop(end) < hop(1 - end))
+        def _():
+            arrive(ya(u))
+        acc[end] = acc[end] + decoded(yrecv_a[u, end], yrscale_a[u, end])
 
         @pl.when(hop(end) > 0)
         def _():
@@ -234,7 +237,13 @@
                 def _():
                     a_y(j, (i - first) * several + q)
             advance(i)
-        each(s, s + steps, both)
+        if j:
+            each(s, s + steps, both)
+        else:
+            both(0)
+            for copy in x_copies[2:]:
+                copy.wait()
+            each(1, steps, both)
         s += steps
     pl.when(at_end)(lambda: each(0, -(-held // 2), lambda u: start(yb(u))))
     each(s, items_b + units_a + LAG * (nz - 1), advance)
@@ -248,6 +257,32 @@
     end_of = z // max(nz - 1, 1)
     mine = dp_at(end_of, y) * rows
 
+    size = rows // PIECES
+    chunks = 2 * PIECES - CROSSING
+
+    def segment(end, yi, chunk):
+        return out_ref.at[pl.ds(pl.multiple_of(dp_at(end, yi) * rows + chunk * size, size), size), :]
+
+    def early(i):
+        ref = segment(end_of, y, i)
+        return remote(ref, ref, yhs_sem.at[i], yhr_sem.at[i], partner)
+
+    def settle():
+        def sent(copies):
+            for copy in copies:
+                copy.wait_send()
+
+        for j in range(1, tasks):
+            c_remote(j).wait_send()
+        each(0, units_a, lambda u: sent(ya(u)))
+        for end in (0, 1):
+            @pl.when(hop(end) < nz - 1)
+            def _():
+                each(0, units_a, lambda u: sent(za(u, end)))
+                each(0, items_b, lambda i: sent(zb(i, end)))
+
+    pl.when(jnp.logical_not(at_end))(settle)
+
     def weigh():
         each(0, units_b, finish_b)
         pairs = [(s, t) for s in range(tasks) for t in range(s, tasks)]
@@ -260,34 +295,41 @@
         sums = lax.fori_loop(0, blocks, products, tuple(jnp.zeros((8, width), jnp.float32) for _ in pairs))
         line = lax.broadcasted_iota(jnp.int32, (8, 128), 0)
         lane = lax.broadcasted_iota(jnp.int32, (8, 128), 1)
-        gram = jnp.zeros((8, 128), jnp.float32)
-        for total, (s, t) in zip(sums, pairs):
+        spot = lane[:1]
+        row = jnp.zeros((1, 128), jnp.float32)
+        for place, total in enumerate(sums):
             value = jnp.sum(jnp.sum(total, axis=0, keepdims=True), axis=1, keepdims=True)
-            here = ((line == s) & (lane == t)) | ((line == t) & (lane == s))
-            gram = gram + jnp.where(here, value, 0.0)
+            row = row + jnp.where(spot == place, value, 0.0)
 
         def peer(k):
             end = k // 2 % 2
             return (lax.rem(me_t + k // 4, tasks), dp_at(nz - 1 - z if end else z, 1 - y if k % 2 else y))
 
-        gram_own[...] = gram
+        gram_own[...] = row
         copies = [remote(gram_own, gram_all.at[k], gs_sem.at[k], gr_sem.at[k], peer(k)) for k in range(1, 4 * tasks)]
         start(copies)
+        settle()
+        for u in range(units_b):
+            for copy in yb(u):
+                copy.wait_send()
         for k, copy in enumerate(copies, 1):
             copy.wait_recv()
-            gram = gram + gram_all[k]
-        for copy in copies:
-            copy.wait_send()
-
+            row = row + gram_all[k]
+
+        gram = jnp.zeros((8, 128), jnp.float32)
+        for place, (s, t) in enumerate(pairs):
+            value = jnp.sum(jnp.where(spot == place, row, 0.0), axis=1, keepdims=True)
+            here = ((line == s) & (lane == t)) | ((line == t) & (lane == s))
+            gram = gram + jnp.where(here, value, 0.0)
         cols = [jnp.sum(jnp.where(lane == m, gram, 0.0), axis=1, keepdims=True) for m in range(tasks)]
         entry = lambda column, i: jnp.sum(jnp.where(line[:, :1] == i, column, 0.0), axis=0, keepdims=True)
-        row = line[:, :1]
-        coefficients = [(row == m).astype(jnp.float32) for m in range(tasks)]
+        rank = line[:, :1]
+        coefficients = [(rank == m).astype(jnp.float32) for m in range(tasks)]
         flag_cols = []
         for m in range(tasks):
             column = jnp.zeros((8, 1), jnp.float32)
             for i in range(tasks):
-                column = column + jnp.where(row == i, flags_ref[i, m].astype(jnp.float32), 0.0)
+                column = column + jnp.where(rank == i, flags_ref[i, m].astype(jnp.float32), 0.0)
             flag_cols.append(column)
         for position in range(tasks):
             target = order_ref[position]
@@ -295,24 +337,23 @@
             column = sum(cols[m] * picks[m] for m in range(tasks))
             dots = sum(coefficients[m] * entry(column, m) for m in range(tasks))
             square = sum(entry(column, m) * picks[m] for m in range(tasks))
-            active = sum(flag_cols[m] * picks[m] for m in range(tasks)) * jnp.where(row == target, 0.0, 1.0)
+            active = sum(flag_cols[m] * picks[m] for m in range(tasks)) * jnp.where(rank == target, 0.0, 1.0)
             removed = jnp.minimum(dots, 0.0) / square * active
             coefficients = [coefficients[m] - removed * picks[m] for m in range(tasks)]
         weights = [jnp.sum(coefficients[m], axis=0, keepdims=True) for m in range(tasks)]
 
-        def mix(index, carry):
+        def mix(index):
             mixed = sum(weights[t] * grads[t, index] for t in range(tasks))
             out_ref[pl.ds(pl.multiple_of(mine + index * step, step), step), :] = mixed.astype(jnp.bfloat16)
-            return carry
-        lax.fori_loop(0, blocks, mix, 0)
+
+        first = CROSSING * blocks // PIECES
+        each(first, blocks, mix)
+        each(CROSSING, PIECES, lambda i: early(i).start())
+        each(0, first, mix)
+        for copy in copies:
+            copy.wait_send()
 
     pl.when(at_end)(weigh)
-
-    size = rows // PIECES
-    chunks = 2 * PIECES - CROSSING
-
-    def segment(end, yi, chunk):
-        return out_ref.at[pl.ds(pl.multiple_of(dp_at(end, yi) * rows + chunk * size, size), size), :]
 
     def along(end, i):
         chunk = jnp.where(i < PIECES, i, i - PIECES + CROSSING)
@@ -322,14 +363,6 @@
     def over(end, i):
         ref = segment(end, y, i)
         return remote(ref, ref, ygs_sem.at[end, i], ygr_sem.at[end, i], partner)
-
-    def early(i):
-        ref = segment(end_of, y, i)
-        return remote(ref, ref, yhs_sem.at[i], yhr_sem.at[i], partner)
-
-    @pl.when(at_end)
-    def _():
-        each(CROSSING, PIECES, lambda i: early(i).start())
 
     def spread(s):
         for end in (0, 1):
@@ -366,23 +399,9 @@
     def _():
         each(CROSSING, PIECES, lambda i: early(i).wait_send())
 
-    for j in range(1, tasks):
-        c_remote(j).wait_send()
-
-    def sent(copies):
-        for copy in copies:
-            copy.wait_send()
-
-    def close_y(u):
-        for end in (0, 1):
-            sent(ya(u, end))
-    each(0, units_a, close_y)
-    pl.when(at_end)(lambda: each(0, units_b, lambda u: sent(yb(u))))
     for end in (0, 1):
         @pl.when(hop(end) < nz - 1)
         def _():
-            each(0, units_a, lambda u: sent(za(u, end)))
-            each(0, items_b, lambda i: sent(zb(i, end)))
             each(0, chunks, lambda i: along(1 - end, i).wait_send())
 
 
@@ -410,9 +429,9 @@
             vmem((2 * nb, 2, *code), i16), vmem((2 * nb, 2, *scale), f32),
             vmem((2 * nb, 2, *code), i16), vmem((2 * nb, 2, *scale), f32),
             vmem((tasks, blocks, step, width), f32),
-            vmem((8, 128), f32), vmem((4 * tasks, 8, 128), f32),
+            vmem((1, 128), f32), vmem((4 * tasks, 1, 128), f32),
             dma((4,)), dma, dma((tasks,)), dma((tasks,)),
-            dma((na, 2, 2)), dma((na, 2, 2)), dma((na, 2, 2)), dma((na, 2, 2)),
+            dma((na, 2)), dma((na, 2)), dma((na, 2, 2)), dma((na, 2, 2)),
             dma((nb, 2)), dma((nb, 2)), dma((2 * nb, 2, 2)), dma((2 * nb, 2, 2)),
             dma((4 * tasks,)), dma((4 * tasks,)),
             dma((2, chunks)), dma((2, chunks)), dma((2, CROSSING)), dma((2, CROSSING)), dma((PIECES,)), dma((PIECES,)),

time: 122 us -> 120 us (0.984)
  Pallas kernels: 120 us -> 118 us
    pallas_call x1, Pallas kernels: 120 us -> 118 us  [on_device(): pl.pallas_call(functools.partial(kernel, tasks, ndp, blocks), out_shape=j...]
where the time goes in v4:
time: 120 us
  Pallas kernels  118 us (98%)
  local copies, waits for them, and re-layouts  1.32 us (1%)
    pallas_call x1, Pallas kernels, on_device(): pl.pallas_call(functools.partial(kernel, tasks, ndp, blocks), out_shape=j...  118 us

profile of v4, /device:TPU:0, one launch (start us, length us, event | category | flops | bytes accessed | tf_op | source)
XLA Modules:
  0.0 119.5 jit_solution(16321709879924535939)
XLA Ops:
  0.0 118.2 %shard_map.46 = bf16[4096,256]{1,0:T(8,128)(2,1)S(1)} custom-call(s32[4]{0:T(128)} %order_ref.1, s32[4,4]{1,0:T(4,128)} %flags_ref.1, bf16[1024,4096]{1,0:T(8,128)(2,1)} %x_hbm.1, bf16[1024,1024]{1,0:T(8,128)(2,1)} %bitcast.1), custom_call_target="tpu_custom_call" | custom-call | tf_op jit(solution)/shard_map/pallas_call | solution.py:442
  118.2 1.3 %copy.6 = bf16[4096,256]{1,0:T(8,128)(2,1)} copy(bf16[4096,256]{1,0:T(8,128)(2,1)S(1)} %shard_map.46) | data formatting | bytes 4194304

commit v5 on v4

--- a/solution.py
+++ b/solution.py
@@ -10,7 +10,8 @@
 MESH = pl.DeviceIdType.MESH
 TOP = 32767.0
 LAG = 3
-SHARE = 12
+PARTS = 1
+SHARE = 13
 REACH = 5
 PIECES = 16
 CROSSING = 12
@@ -26,16 +27,16 @@
     return code.astype(jnp.int32).astype(jnp.float32) * scale
 
 
-def shares(blocks):
-    low = blocks * SHARE // 32
-    return low, blocks * SHARE // 16 - low
-
-
-def kernel(tasks, ndp, blocks, order_ref, flags_ref, x_hbm, c_hbm, out_ref,
-           x_ref, cots, acc, ysend_a, yscale_a, yrecv_a, yrscale_a, zsend_a, zscale_a, zrecv_a, zrscale_a,
+def shares(tasks, blocks):
+    total = tasks * blocks * SHARE // 32
+    return [(j + 1) * total // tasks - j * total // tasks for j in range(tasks)]
+
+
+def kernel(tasks, ndp, blocks, order_hbm, flags_hbm, x_hbm, c_hbm, out_ref,
+           order_ref, flags_ref, x_ref, cots, acc, ysend_a, yscale_a, yrecv_a, yrscale_a, zsend_a, zscale_a, zrecv_a, zrscale_a,
            ysend_b, yscale_b, yrecv_b, yrscale_b, zsend_b, zscale_b, zrecv_b, zrscale_b,
            grads, gram_own, gram_all,
-           x_sem, c_sem, cs_sem, cr_sem,
+           o_sem, x_sem, c_sem, cs_sem, cr_sem,
            yas_sem, yar_sem, zas_sem, zar_sem, ybs_sem, ybr_sem, zbs_sem, zbr_sem,
            gs_sem, gr_sem, zgs_sem, zgr_sem, ygs_sem, ygr_sem, yhs_sem, yhr_sem):
     nz = ndp // 2
@@ -47,10 +48,10 @@
     step = acc.shape[1]
     width = cots.shape[2]
     rows = step * blocks
-    low_b, high_b = shares(blocks)
-    low_a, high_a = blocks - high_b, blocks - low_b
-    pair_b, pair_a = low_b + high_b, low_a + high_a
-    units_a, units_b = pair_a * pairs_of, pair_b * pairs_of
+    of_b = shares(tasks, blocks)
+    of_a = [blocks - n for n in of_b]
+    base_a, base_b = [[sum(of[:j]) for j in range(tasks)] for of in (of_a, of_b)]
+    units_a, units_b = sum(of_a), sum(of_b)
     at_end = (z == 0) | (z == nz - 1)
 
     def dp_at(zi, yi):
@@ -59,14 +60,17 @@
     def mate(j, way):
         return lax.rem(me_t // 2 + way * (j // 2) + pairs_of, pairs_of) * 2 + lax.rem(me_t % 2 + j % 2, 2)
 
+    def slot(u, base):
+        return sum(jnp.where(u >= first, 1, 0) for first in base[1:])
+
+    def pick(u, base, values):
+        return values[0] + sum(jnp.where(u >= base[j], values[j] - values[j - 1], 0) for j in range(1, tasks))
+
     def place_a(u):
-        r = u % pair_a
-        return u // pair_a * 2 + r // high_a, r % high_a
+        return slot(u, base_a), u - pick(u, base_a, base_a)
 
     def place_b(u):
-        r = u % pair_b
-        odd = (r + high_b - low_b) // high_b
-        return u // pair_b * 2 + odd, r - odd * low_b + high_a - odd * (high_a - low_a)
+        return slot(u, base_b), u - pick(u, base_b, [base_b[j] - of_a[j] for j in range(tasks)])
 
     partner = (me_t, dp_at(z, 1 - y))
 
@@ -88,6 +92,11 @@
     def ahead(end):
         return (me_t, dp_at(jnp.clip(z + (1 if end else -1), 0, nz - 1), y))
 
+    o_copies = [pltpu.make_async_copy(order_hbm, order_ref, o_sem.at[0]),
+                pltpu.make_async_copy(flags_hbm, flags_ref, o_sem.at[1])]
+    for copy in o_copies:
+        copy.start()
+
     barrier = pltpu.get_barrier_semaphore()
     pl.semaphore_signal(barrier, inc=1, device_id=partner, device_id_type=MESH)
     for k in range(1, tasks):
@@ -122,10 +131,10 @@
         return (remote(ysend_b.at[u], yrecv_b.at[u], ybs_sem.at[u, 0], ybr_sem.at[u, 0], partner),
                 remote(yscale_b.at[u], yrscale_b.at[u], ybs_sem.at[u, 1], ybr_sem.at[u, 1], partner))
 
-    def za(u, end):
-        device = ahead(end)
-        return (remote(zsend_a.at[u, end], zrecv_a.at[u, end], zas_sem.at[u, end, 0], zar_sem.at[u, end, 0], device),
-                remote(zscale_a.at[u, end], zrscale_a.at[u, end], zas_sem.at[u, end, 1], zar_sem.at[u, end, 1], device))
+    def za(u, end, h):
+        device, at = ahead(end), (u, end, h)
+        return (remote(zsend_a.at[at], zrecv_a.at[at], zas_sem.at[(*at, 0)], zar_sem.at[(*at, 0)], device),
+                remote(zscale_a.at[at], zrscale_a.at[at], zas_sem.at[(*at, 1)], zar_sem.at[(*at, 1)], device))
 
     def zb(i, end):
         device = ahead(end)
@@ -145,7 +154,7 @@
             lax.fori_loop(first, last, lambda i, carry: (body(i), carry)[1], 0)
 
     def a_y(j, i):
-        u = j // 2 * pair_a + j % 2 * high_a + i
+        u = base_a[j] + i
         for end in (0, 1):
             code, scale = coded(product(j, i, end, 1 - y))
             ysend_a[u, end] = code
@@ -192,21 +201,30 @@
             arrive(ya(u))
         acc[end] = acc[end] + decoded(yrecv_a[u, end], yrscale_a[u, end])
 
-        @pl.when(hop(end) > 0)
-        def _():
-            arrive(za(u, end))
-            acc[end] = acc[end] + decoded(zrecv_a[u, end], zrscale_a[u, end])
-
-        @pl.when(hop(end) < nz - 1)
-        def _():
-            code, scale = coded(acc[end])
-            zsend_a[u, end] = code
-            zscale_a[u, end] = scale
-            start(za(u, end))
+        for h in range(PARTS):
+            part = pl.ds(h * (step // PARTS), step // PARTS)
+
+            @pl.when(hop(end) > 0)
+            def _():
+                arrive(za(u, end, h))
+                acc[end, part] = acc[end, part] + decoded(zrecv_a[u, end, h], zrscale_a[u, end, h])
+
+            @pl.when(hop(end) < nz - 1)
+            def _():
+                code, scale = coded(acc[end, part])
+                zsend_a[u, end, h] = code
+                zscale_a[u, end, h] = scale
+                start(za(u, end, h))
 
         @pl.when(hop(end) == nz - 1)
         def _():
             grads[mate(j, -1), block] = acc[end]
+
+    def finish_b(u):
+        j, block = place_b(u)
+        arrive(yb(u))
+        task = mate(j, -1)
+        grads[task, block] = grads[task, block] + decoded(yrecv_b[u], yrscale_b[u])
 
     items_b = 2 * units_b
     held = max(items_b - LAG * (nz - 1), 0)
@@ -227,8 +245,8 @@
     for j in range(tasks):
         if j:
             c_remote(j).wait_recv()
-        steps = 2 * (high_b if j % 2 else low_b)
-        count = low_a if j % 2 else high_a
+        steps = 2 * of_b[j]
+        count = of_a[j]
         several = -(-count // steps)
 
         def both(i, first=s, j=j, count=count, several=several):
@@ -246,13 +264,18 @@
             each(1, steps, both)
         s += steps
     pl.when(at_end)(lambda: each(0, -(-held // 2), lambda u: start(yb(u))))
-    each(s, items_b + units_a + LAG * (nz - 1), advance)
-
-    def finish_b(u):
-        j, block = place_b(u)
-        arrive(yb(u))
-        task = mate(j, -1)
-        grads[task, block] = grads[task, block] + decoded(yrecv_b[u], yrscale_b[u])
+    total = items_b + units_a + LAG * (nz - 1)
+
+    def last(i):
+        advance(i)
+
+        @pl.when(at_end & (i >= total - units_b))
+        def _():
+            finish_b(i - (total - units_b))
+    each(s, total, last)
+
+    for copy in o_copies:
+        copy.wait()
 
     end_of = z // max(nz - 1, 1)
     mine = dp_at(end_of, y) * rows
@@ -278,13 +301,12 @@
         for end in (0, 1):
             @pl.when(hop(end) < nz - 1)
             def _():
-                each(0, units_a, lambda u: sent(za(u, end)))
+                each(0, units_a, lambda u: [sent(za(u, end, h)) for h in range(PARTS)] and None)
                 each(0, items_b, lambda i: sent(zb(i, end)))
 
     pl.when(jnp.logical_not(at_end))(settle)
 
     def weigh():
-        each(0, units_b, finish_b)
         pairs = [(s, t) for s in range(tasks) for t in range(s, tasks)]
 
         def products(index, sums):
@@ -415,34 +437,35 @@
         step = min(rows, 128)
         blocks = rows // step
         width = cot.shape[1] // tasks
-        nb = sum(shares(blocks)) * (tasks // 2)
+        nb = sum(shares(tasks, blocks))
         na = tasks * blocks - nb
         vmem, dma = pltpu.VMEM, pltpu.SemaphoreType.DMA
         f32, i16, bf16 = jnp.float32, jnp.int16, jnp.bfloat16
         code, scale = (step, width), (1, width)
         chunks = 2 * PIECES - CROSSING
         scratch = [
+            pltpu.SMEM((tasks,), jnp.int32), pltpu.SMEM((tasks, tasks), jnp.int32),
             vmem(inputs.shape, bf16), vmem((tasks, tokens, width), bf16), vmem((2, step, width), f32),
             vmem((na, 2, *code), i16), vmem((na, 2, *scale), f32), vmem((na, 2, *code), i16), vmem((na, 2, *scale), f32),
-            vmem((na, 2, *code), i16), vmem((na, 2, *scale), f32), vmem((na, 2, *code), i16), vmem((na, 2, *scale), f32),
+            vmem((na, 2, PARTS, step // PARTS, width), i16), vmem((na, 2, PARTS, *scale), f32),
+            vmem((na, 2, PARTS, step // PARTS, width), i16), vmem((na, 2, PARTS, *scale), f32),
             vmem((nb, *code), i16), vmem((nb, *scale), f32), vmem((nb, *code), i16), vmem((nb, *scale), f32),
             vmem((2 * nb, 2, *code), i16), vmem((2 * nb, 2, *scale), f32),
             vmem((2 * nb, 2, *code), i16), vmem((2 * nb, 2, *scale), f32),
             vmem((tasks, blocks, step, width), f32),
             vmem((1, 128), f32), vmem((4 * tasks, 1, 128), f32),
-            dma((4,)), dma, dma((tasks,)), dma((tasks,)),
-            dma((na, 2)), dma((na, 2)), dma((na, 2, 2)), dma((na, 2, 2)),
+            dma((2,)), dma((4,)), dma, dma((tasks,)), dma((tasks,)),
+            dma((na, 2)), dma((na, 2)), dma((na, 2, PARTS, 2)), dma((na, 2, PARTS, 2)),
             dma((nb, 2)), dma((nb, 2)), dma((2 * nb, 2, 2)), dma((2 * nb, 2, 2)),
             dma((4 * tasks,)), dma((4 * tasks,)),
             dma((2, chunks)), dma((2, chunks)), dma((2, CROSSING)), dma((2, CROSSING)), dma((PIECES,)), dma((PIECES,)),
         ]
-        smem = pl.BlockSpec(memory_space=pltpu.SMEM)
         whole = pl.BlockSpec(memory_space=pltpu.VMEM)
         hbm = pl.BlockSpec(memory_space=pltpu.HBM)
         return pl.pallas_call(
             functools.partial(kernel, tasks, ndp, blocks),
             out_shape=jax.ShapeDtypeStruct((inputs.shape[1], width), jnp.bfloat16),
-            in_specs=[smem, smem, hbm, hbm],
+            in_specs=[hbm] * 4,
             out_specs=whole,
             scratch_shapes=scratch,
             compiler_params=pltpu.CompilerParams(collective_id=0, has_side_effects=True,

time: 120 us -> 118 us (0.983)
  Pallas kernels: 118 us -> 116 us
    pallas_call x1, Pallas kernels: 118 us -> 116 us  [on_device(): pl.pallas_call(functools.partial(kernel, tasks, ndp, blocks), out_shape=j...]
where the time goes in v5:
time: 118 us; the launch traced here: 117 us
  Pallas kernels  116 us (98%)
  local copies, waits for them, and re-layouts  1.32 us (1%)
    pallas_call x1, Pallas kernels, on_device(): pl.pallas_call(functools.partial(kernel, tasks, ndp, blocks), out_shape=j...  116 us

profile of v5, /device:TPU:0, one launch (start us, length us, event | category | flops | bytes accessed | tf_op | source)
XLA Modules:
  0.0 117.5 jit_solution(7517639616381004703)
XLA Ops:
  0.0 116.2 %shard_map.46 = bf16[4096,256]{1,0:T(8,128)(2,1)S(1)} custom-call(s32[4]{0:T(128)} %order_hbm.1, s32[4,4]{1,0:T(4,128)} %flags_hbm.1, bf16[1024,4096]{1,0:T(8,128)(2,1)} %x_hbm.1, bf16[1024,1024]{1,0:T(8,128)(2,1)} %bitcast.1), custom_call_target="tpu_custom_call" | custom-call | tf_op jit(solution)/shard_map/pallas_call | solution.py:465
  116.2 1.3 %copy.6 = bf16[4096,256]{1,0:T(8,128)(2,1)} copy(bf16[4096,256]{1,0:T(8,128)(2,1)S(1)} %shard_map.46) | data formatting | bytes 4194304

commit v6 on v5

--- a/solution.py
+++ b/solution.py
@@ -142,7 +142,7 @@
                 remote(zscale_b.at[i, end], zrscale_b.at[i, end], zbs_sem.at[i, end, 1], zbr_sem.at[i, end, 1], device))
 
     def start(copies):
-        for copy in copies:
+        for copy in reversed(copies):
             copy.start()
 
     def arrive(copies):
@@ -157,8 +157,8 @@
         u = base_a[j] + i
         for end in (0, 1):
             code, scale = coded(product(j, i, end, 1 - y))
+            yscale_a[u, end] = scale
             ysend_a[u, end] = code
-            yscale_a[u, end] = scale
         start(ya(u))
 
     def b_z(i, end):
@@ -174,15 +174,15 @@
         @pl.when(hop(end) < nz - 1)
         def _():
             code, scale = coded(acc[end])
+            zscale_b[i, end] = scale
             zsend_b[i, end] = code
-            zscale_b[i, end] = scale
             start(zb(i, end))
 
         @pl.when((hop(end) == nz - 1) & (p == 0))
         def _():
             code, scale = coded(acc[end])
+            yscale_b[u] = scale
             ysend_b[u] = code
-            yscale_b[u] = scale
 
             @pl.when(i >= held)
             def _():
@@ -212,8 +212,8 @@
             @pl.when(hop(end) < nz - 1)
             def _():
                 code, scale = coded(acc[end, part])
+                zscale_a[u, end, h] = scale
                 zsend_a[u, end, h] = code
-                zscale_a[u, end, h] = scale
                 start(za(u, end, h))
 
         @pl.when(hop(end) == nz - 1)

time: 118 us -> 117 us (level)
  no operation moved by 1% of the time
where the time goes in v6:
time: 117 us
  Pallas kernels  116 us (99%)
  local copies, waits for them, and re-layouts  1.32 us (1%)
    pallas_call x1, Pallas kernels, on_device(): pl.pallas_call(functools.partial(kernel, tasks, ndp, blocks), out_shape=j...  116 us

profile of v6, /device:TPU:0, one launch (start us, length us, event | category | flops | bytes accessed | tf_op | source)
XLA Modules:
  0.0 117.3 jit_solution(13670473698112083421)
XLA Ops:
  0.0 116.0 %shard_map.46 = bf16[4096,256]{1,0:T(8,128)(2,1)S(1)} custom-call(s32[4]{0:T(128)} %order_hbm.1, s32[4,4]{1,0:T(4,128)} %flags_hbm.1, bf16[1024,4096]{1,0:T(8,128)(2,1)} %x_hbm.1, bf16[1024,1024]{1,0:T(8,128)(2,1)} %bitcast.1), custom_call_target="tpu_custom_call" | custom-call | tf_op jit(solution)/shard_map/pallas_call | solution.py:465
  116.0 1.3 %copy.6 = bf16[4096,256]{1,0:T(8,128)(2,1)} copy(bf16[4096,256]{1,0:T(8,128)(2,1)S(1)} %shard_map.46) | data formatting | bytes 4194304
